TPU v7x, 128 devices: a whole 4x4x4 slice. The times are simulated.
128 devices in a mesh: dp: 8 (over z_lo, y), tensor: 16 (over z_hi, x, core).
Axes of the slice: x: 4, y: 4, z: 4 (z_hi: 2, z_lo: 2; z = z_hi * 2 + z_lo), core: 2. Of those that a mesh axis runs over, the one named last changes fastest.
Arguments:
- token_ids: int32 [4096], P('dp'), may hold values from 0 to 76031
- positions: int32 [4096], P('dp'), may hold values from 0 to 511, as said below
- embed_table: bfloat16 [76032, 8192], P('dp', 'tensor'), may hold values from -6 to 6
- norm_gain: float32 [8192], replicated, may hold values from 0.25 to 1.75
- wq: bfloat16 [8192, 8192], P(('dp', 'tensor')), may hold values from -1 to 1, as said below
- wk: bfloat16 [8192, 1024], P(('dp', 'tensor')), may hold values from -8 to 8, as said below
- wv: bfloat16 [8192, 1024], P(('dp', 'tensor')), may hold values from -0.0625 to 0.0625
Outputs:
- attended: bfloat16 [4096, 8192], P('dp', 'tensor')
Inputs may be any that keep to these rules, and one draw needn't show every extreme that they name: `positions`: a position is 0 exactly where a prompt starts and otherwise one more than the previous token's; the first token of each block of 512 starts a prompt; in some block a single prompt fills all 512 tokens. `wq`: a weight matrix. `wk`: a weight matrix.
All inputs are finite; a program needn't handle non-finite values.
Results may differ from a plain program's by a relative error of at most 0.0025.
The roundings to bfloat16 on the way count: a program that leaves them out, or rounds other values in their place, can miss the bound.
Values may be sent and summed in bfloat16 or wider, within the bound.
A program may use at most 128 MiB of HBM per device.

v0:
```python
import jax
import jax.numpy as jnp
from jax import lax
from jax.sharding import Mesh
from jax.sharding import PartitionSpec as P

KEY_VALUE_HEADS = 8
HEAD_SIZE = 128
DP = ("dp_0", "dp_1")
DP_TENSOR = ("dp_0", "dp_1", "tensor")


def laid_out(pieces, dim):
    pieces = jnp.moveaxis(pieces, 0, dim)
    lengths = pieces.shape
    return pieces.reshape(*lengths[:dim], lengths[dim] * lengths[dim + 1], *lengths[dim + 2 :])


def from_everyone(x, axis):
    count = lax.axis_size(axis)
    return lax.all_to_all(jnp.broadcast_to(x[None], (count, *x.shape)), axis, 0, 0, tiled=True)


def gathered_copies(x, axis, dim):
    return laid_out(from_everyone(x, axis), dim)


def gather_in_order(x, axes, sequence):
    pieces = x[None]
    for k in sequence:
        pieces = lax.all_gather(pieces, axes[k], axis=0, tiled=True)
    held = [lax.axis_size(axes[k]) for k in reversed(sequence)]
    pieces = pieces.reshape(*held, *x.shape)
    turned = sorted(range(len(sequence)), key=lambda place: sequence[len(sequence) - 1 - place])
    return pieces.transpose(*turned, *range(len(sequence), pieces.ndim)).reshape(-1, *x.shape)


def whole_of(x, axes, sequence, dim):
    return laid_out(gather_in_order(x, axes, sequence), dim)


def rotate(vectors, positions):
    half_dim = vectors.shape[-1] // 2
    frequency = 1000000.0 ** (-(jnp.arange(half_dim, dtype=jnp.float32) * 2.0 / vectors.shape[-1]))
    angles = positions.astype(jnp.float32)[:, None] * frequency[None, :]
    cosine = jnp.cos(angles)[:, None, :]
    sine_term = jnp.sin(angles)[:, None, :]
    lower_half = vectors[..., :half_dim]
    upper_half = vectors[..., half_dim:]
    return jnp.concatenate(
        [
            lower_half * cosine - upper_half * sine_term,
            upper_half * cosine + lower_half * sine_term,
        ],
        axis=-1,
    )


def on_device(token_ids, positions, embed_table, norm_gain, wq, wk, wv):
    tokens = token_ids.shape[0]
    every_id = gathered_copies(token_ids, DP, 0)
    vocab_rows = embed_table.shape[0]
    offset = lax.axis_index(DP) * vocab_rows
    local_ids = every_id - offset
    inside = (local_ids >= 0) & (local_ids < vocab_rows)
    picked = jnp.take(embed_table, jnp.clip(local_ids, 0, vocab_rows - 1), axis=0)
    partial_value = jnp.where(inside[:, None], picked, jnp.zeros_like(picked))
    embedded = (
        lax.psum_scatter(partial_value, DP, scatter_dimension=0, tiled=True)
        .astype(jnp.float32)
        .astype(jnp.bfloat16)
    )
    features = lax.all_gather(embedded, "tensor", axis=1, tiled=True)
    hidden = features.astype(jnp.float32)
    mean_square = jnp.mean(hidden * hidden, axis=-1, keepdims=True)
    normed_hidden = (hidden * lax.rsqrt(mean_square + 1e-06) * norm_gain[None, :]).astype(
        jnp.bfloat16
    )
    tensor_parallel_count = lax.axis_size("tensor")
    repeat_factor = tensor_parallel_count // KEY_VALUE_HEADS
    sharded_row_block = wq.shape[0]
    query_cols = wq.shape[1] // tensor_parallel_count
    per_owner = query_cols + 2 * HEAD_SIZE
    key_portion_rows = jnp.repeat(
        wk.reshape(sharded_row_block, KEY_VALUE_HEADS, HEAD_SIZE), repeat_factor, axis=1
    )
    value_portion_rows = jnp.repeat(
        wv.reshape(sharded_row_block, KEY_VALUE_HEADS, HEAD_SIZE), repeat_factor, axis=1
    )
    combined = jnp.concatenate(
        [
            wq.reshape(sharded_row_block, tensor_parallel_count, query_cols),
            key_portion_rows,
            value_portion_rows,
        ],
        axis=2,
    )
    combined = combined.reshape(sharded_row_block, tensor_parallel_count * per_owner)
    owner_rows = lax.all_to_all(combined, "tensor", split_axis=1, concat_axis=0, tiled=True)
    projected = jnp.dot(
        normed_hidden, whole_of(owner_rows, DP, (0, 1), 0), preferred_element_type=jnp.float32
    )
    head_count = query_cols // HEAD_SIZE
    query_tensor = rotate(
        projected[:, :query_cols].reshape(tokens, head_count, HEAD_SIZE), positions
    ).astype(jnp.bfloat16)
    key_row_block = rotate(
        projected[:, query_cols : query_cols + HEAD_SIZE].reshape(tokens, 1, HEAD_SIZE), positions
    )[:, 0, :].astype(jnp.bfloat16)
    value_tensor = projected[:, query_cols + HEAD_SIZE :].astype(jnp.bfloat16)
    scale = 1.0 / HEAD_SIZE**0.5
    scores = (
        jnp.einsum("qhd,kd->hqk", query_tensor, key_row_block, preferred_element_type=jnp.float32)
        * scale
    )
    places = jnp.arange(tokens, dtype=jnp.int32)
    allowed = (places[None, :] <= places[:, None]) & (
        positions[:, None] - positions[None, :] == places[:, None] - places[None, :]
    )
    scores = jnp.where(allowed[None, :, :], scores, -1e30)
    largest = jnp.max(scores, axis=-1, keepdims=True)
    exponent = jnp.where(allowed[None, :, :], jnp.exp(scores - largest), 0.0)
    probs = (exponent / jnp.sum(exponent, axis=-1, keepdims=True)).astype(jnp.bfloat16)
    attended = jnp.einsum(
        "hqk,kd->qhd", probs, value_tensor, preferred_element_type=jnp.float32
    ).astype(jnp.bfloat16)
    return attended.reshape(tokens, query_cols)


def solution(mesh):
    finer = Mesh(mesh.devices.reshape(2, 4, mesh.shape["tensor"]), ("dp_0", "dp_1", "tensor"))
    placed = (
        P(DP),
        P(DP),
        P(DP, "tensor"),
        P(),
        P(DP_TENSOR, None),
        P(DP_TENSOR, None),
        P(DP_TENSOR, None),
    )
    return jax.shard_map(
        on_device, mesh=finer, in_specs=placed, out_specs=P(DP, "tensor"), check_vma=False
    )
```

profile of v0, /device:TPU:0, one launch (start us, length us, event | category | flops | bytes accessed | tf_op | source)
XLA Modules:
  0.0 343.1 jit_solution(15538614825886746059)
XLA Ops:
  7.4 0.9 copy.61
  8.3 0.9 copy.60
  9.2 1.6 copy.59
  10.8 0.2 broadcast_in_dim.81
  11.0 0.2 broadcast_in_dim.80
  11.3 0.5 copy.41
  11.8 31.3 %all_to_all.19 = bf16[64,16,768]{2,0,1:T(8,128)(2,1)} all-to-all(bf16[64,16,768]{2,0,1:T(8,128)(2,1)S(1)} %copy.41), channel_id=1, replica_groups=mesh['dp_0'=2,'dp_1'=4,'tensor'=16] {'tensor'}, dimensions={1} | all-to-all | bytes 3145728 | tf_op jit(solution)/shard_map/all_to_all | solution.py:99
  43.1 0.6 broadcast_in_dim.46
  43.7 4.9 %all-to-all-start = ((s32[8,1,512]{2,1,0:T(1,128)}), s32[8,1,512]{2,1,0:T(1,128)S(1)}, u32[]{:S(2)}, u32[]{:S(2)}) async-start(s32[8,1,512]{2,1,0:T(1,128)} %broadcast_in_dim.46), calls=%async_computation | async-start | bytes 32768 | tf_op jit(solution)/shard_map/all_to_all | solution.py:21
  48.7 6.2 %all-to-all-done = s32[8,1,512]{2,1,0:T(1,128)S(1)} async-done(((s32[8,1,512]{2,1,0:T(1,128)}), s32[8,1,512]{2,1,0:T(1,128)S(1)}, u32[]{:S(2)}, u32[]{:S(2)}) %all-to-all-start) | async-done | bytes 16416 | tf_op jit(solution)/shard_map/all_to_all | solution.py:21
  55.0 22.4 %gather_fusion = bf16[4096,512]{1,0:T(8,128)(2,1)} fusion(bf16[9504,512]{1,0:T(8,128)(2,1)} %param.9, s32[4096]{0:T(1024)S(1)} %broadcast_clamp_fusion), kind=kCustom, calls=%fused_computation | custom fusion | bytes 8404992 | tf_op jit(solution)/shard_map/jit(_take)/gather | solution.py:66
  77.4 5.3 %select_select_fusion = bf16[4096,512]{1,0:T(8,128)(2,1)} fusion(bf16[4096,512]{1,0:T(8,128)(2,1)} %gather_fusion, pred[4096]{0:T(1024)(128)(4,1)S(1)} %compare_and_fusion, pred[4096]{0:T(1024)(128)(4,1)S(1)} %bitcast.60), kind=kLoop, calls=%fused_computation.13 | loop fusion | flops 4194304 | bytes 8396800 | tf_op jit(solution)/shard_map/jit(_where)/select_n | solution.py:67
  82.8 5.0 %all-gather.6.cloned.1.call-done = bf16[2,1024,768]{2,1,0:T(8,128)(2,1)} async-done(((bf16[1,1024,768]{2,1,0:T(8,128)(2,1)}), bf16[2,1024,768]{2,1,0:T(8,128)(2,1)}) %all-gather.6.cloned.1.call-update) | async-done | bytes 3145744 | tf_op jit(solution)/shard_map/all_gather | solution.py:31
  87.8 0.2 all-gather.4.cloned.1.call-start
  88.0 145.3 %reduce-scatter.2.cloned.1.call-done = bf16[512,512]{1,0:T(8,128)(2,1)} async-done(((bf16[4096,512]{1,0:T(8,128)(2,1)}), bf16[512,512]{1,0:T(8,128)(2,1)}) %reduce-scatter.2.cloned.1.call-update) | async-done | bytes 524304 | tf_op jit(solution)/shard_map/reduce_scatter | solution.py:69
  233.4 1.0 fusion.14
  234.4 1.8 multiply_cosine_fusion
  236.2 10.8 %copy.42 = bf16[2,4,1024,768]{3,2,1,0:T(8,128)(2,1)} copy(bf16[2,4,1024,768]{3,2,0,1:T(8,128)(2,1)} %bitcast.44) | data formatting | bytes 25165824 | tf_op jit(solution)/shard_map/transpose | solution.py:35
  247.0 64.4 %all-gather.4.cloned.1.call-done = bf16[512,8192]{1,0:T(8,128)(2,1)} async-done(((bf16[512,512]{1,0:T(8,128)(2,1)}), bf16[512,8192]{1,0:T(8,128)(2,1)}) %all-gather.4.cloned.1.call-update) | async-done | bytes 8388624 | tf_op jit(solution)/shard_map/all_gather | solution.py:73
  311.4 5.3 %fusion.1 = f32[512]{0:T(512)S(1)} fusion(bf16[512,8192]{1,0:T(8,128)(2,1)} %all-gather.4.cloned.1.call-done), kind=kLoop, calls=%fused_computation.4 | loop fusion | flops 12582400 | bytes 8390656 | tf_op jit(solution)/shard_map/reduce_sum | solution.py:75
  316.7 0.5 copy-done
  317.2 9.9 %fusion.4 = f32[512,768]{1,0:T(8,128)S(1)} fusion(bf16[8192,768]{1,0:T(8,128)(2,1)} %bitcast.45, bf16[512,8192]{1,0:T(8,128)(2,1)S(1)} %copy-done, f32[8192]{0:T(1024)S(1)} %copy-done.6, f32[512]{0:T(512)S(1)} %add_rsqrt_fusion), kind=kOutput, calls=%fused_computation.7 | convolution fusion | flops 6459228160 | bytes 22579200 | tf_op jit(solution)/shard_map/dot_general | solution.py:100
  327.1 0.1 slice.35
  327.2 1.0 copy-done.1
  328.2 0.4 reshape.261
  328.6 0.6 fusion.34
  329.4 0.6 fusion.24
  329.9 1.3 subtract_convert_fusion
  331.3 0.8 fusion.15
  332.1 2.4 fusion.35
  334.5 0.5 fusion.13
  335.0 1.0 copy.49
  (33 shorter events, 0.6 us)
Async XLA Ops:
  7.4 80.4 %all-gather.6.cloned.1.call-start = ((), (), s32[]{:S(2)}) async-start(), calls=%async_computation.5 | async-start | bytes 4718592 | tf_op jit(solution)/shard_map/all_gather | solution.py:31
  11.3 31.8 %copy-start.5 = (s32[512]{0:T(512)S(1)}, s32[512]{0:T(512)}, u32[]{:S(2)}) copy-start(s32[512]{0:T(512)} %param.7) | copy-start | bytes 6148
  43.7 11.1 %all-to-all-start = ((s32[8,1,512]{2,1,0:T(1,128)}), s32[8,1,512]{2,1,0:T(1,128)S(1)}, u32[]{:S(2)}, u32[]{:S(2)}) async-start(s32[8,1,512]{2,1,0:T(1,128)} %broadcast_in_dim.46), calls=%async_computation | async-start | bytes 32768 | tf_op jit(solution)/shard_map/all_to_all | solution.py:21
  48.6 184.7 %reduce-scatter.2.cloned.1.call-start = ((), (), s32[]{:S(2)}) async-start(), calls=%async_computation.3 | async-start | bytes 4718592 | tf_op jit(solution)/shard_map/reduce_scatter | solution.py:69
  82.7 150.7 %copy-start.4 = (s32[512]{0:T(512)S(1)}, s32[512]{0:T(512)}, u32[]{:S(2)}) copy-start(s32[512]{0:T(512)} %param.8) | copy-start | bytes 6148
  82.7 153.5 %all-gather.8.cloned.1.call-start = ((), (), s32[]{:S(2)}) async-start(), calls=%async_computation.6 | async-start | bytes 15728640 | tf_op jit(solution)/shard_map/all_gather | solution.py:31
  87.8 223.7 %all-gather.4.cloned.1.call-start = ((), (), s32[]{:S(2)}) async-start(), calls=%async_computation.4 | async-start | bytes 8912896 | tf_op jit(solution)/shard_map/all_gather | solution.py:73
  236.2 80.5 %copy-start.6 = (f32[8192]{0:T(1024)S(1)}, f32[8192]{0:T(1024)}, u32[]{:S(2)}) copy-start(f32[8192]{0:T(1024)} %param.10) | copy-start | bytes 98308
  311.4 5.8 %copy-start = (bf16[512,8192]{1,0:T(8,128)(2,1)S(1)}, bf16[512,8192]{1,0:T(8,128)(2,1)}, u32[]{:S(2)}) copy-start(bf16[512,8192]{1,0:T(8,128)(2,1)} %all-gather.4.cloned.1.call-done) | copy-start | bytes 25165828
  327.1 1.2 copy-start.1
  328.2 1.0 slice-start
  329.9 2.2 copy-start.3
  332.1 2.4 copy-start.2
Sparse Core Ops, SparseCore 0:
  43.2 44.5 all-gather.5
  89.4 134.1 all-gather.7
  233.5 77.8 all-gather.3
Sparse Core Ops, SparseCore 1:
  82.8 150.5 reduce-scatter.1
where the time goes:
time: 345 us; the launch traced here: 343 us
  waiting for transfers between devices  221 us (64%)
  local copies, waits for them, and re-layouts  41.9 us (12%)
  blocking collectives  31.3 us (9%)
  other arithmetic  17.8 us (5%)
  between operations  14.8 us (4%)
  matrix products  11.1 us (3%)
  starting transfers between devices  5.23 us (2%)
    reduce_scatter x1, waiting for transfers between devices, on_device(): lax.psum_scatter(partial_value, DP, scatter_dimension=0, tiled=True)  145 us
    all_gather x1, waiting for transfers between devices, on_device(): features = lax.all_gather(embedded, 'tensor', axis=1, tiled=True)  64.4 us
    all_to_all x1, blocking collectives, on_device(): lax.all_to_all(combined, 'tensor', split_axis=1, concat_axis=0, tiled=True)  31.3 us
    gather x1, local copies, waits for them, and re-layouts, on_device(): jnp.take(embed_table, jnp.clip(local_ids, 0, vocab_rows - 1), axis=0)  22.4 us
    transpose x1, local copies, waits for them, and re-layouts, gather_in_order(): pieces.transpose(*turned, *range(len(sequence), pieces.ndim))  10.8 us
    dot_general x1, matrix products, on_device(): jnp.dot(normed_hidden, whole_of(owner_rows, DP, (0, 1), 0), preferred_ele...  9.86 us
  transfers between devices with their start and end apart: 5, of which 4 were waited for; matrix products, arithmetic and copies ran while one was open for 12% of the time, Pallas kernels for 0%

commit v1 on v0

v1 whole, which is shorter than its diff:
```python
import jax
import jax.numpy as jnp
from jax import lax
from jax.experimental import pallas as pl
from jax.experimental.pallas import tpu as pltpu
from jax.sharding import PartitionSpec as P

MESH = pl.DeviceIdType.MESH
F32, BF16, I32 = jnp.float32, jnp.bfloat16, jnp.int32
TOK = 512
PART = 256
ROWS = 9504
HEAD = 128
TAB_COPIES = 6
NEG = -1e30


def kernel(
    ids, cosine, sine, first_col, first_row, gain, table, wq, wk, wv, out,
    landed, tab, stage, ids_all, index_v, index_s, mine, half_in, final_in,
    zsend, zrecv, acts, normed, wa, wb, psa, pra, psb, prb, acca, accb, kv,
    sq, sq_own, sq_in, inv,
    ids_ss, ids_rs, tab_sem, sm_sem, x_ss, x_rs, g_ss, h_rs, f_rs, z_ss, z_rs,
    a_ss, a_rs, q_ss, q_rs, w_ss, wa_rs, wb_rs, p_ss, p_rs, kv_ss, kv_rs,
):
    d = lax.axis_index("dp")
    t = lax.axis_index("tensor")
    zl, y = d // 4, lax.rem(d, 4)
    h, x, k = t // 8, lax.rem(t // 2, 4), lax.rem(t, 2)
    yp, y2, ym = lax.rem(y + 1, 4), lax.rem(y + 2, 4), lax.rem(y + 3, 4)
    xp, x2, xm = lax.rem(x + 1, 4), lax.rem(x + 2, 4), lax.rem(x + 3, 4)
    up, down, over = (zl * 4 + yp, t), (zl * 4 + ym, t), ((1 - zl) * 4 + y, t)

    def slot(hh, xx, kk):
        return hh * 8 + xx * 2 + kk

    started = []

    def send(src, dst, ss, rs, device):
        copy = pltpu.make_async_remote_copy(
            src_ref=src, dst_ref=dst, send_sem=ss, recv_sem=rs, device_id=device, device_id_type=MESH
        )
        copy.start()
        started.append(copy)

    def arrived(dst, ss, rs):
        pltpu.make_async_remote_copy(
            src_ref=dst, dst_ref=dst, send_sem=ss, recv_sem=rs, device_id=over, device_id_type=MESH
        ).wait_recv()

    part = ROWS // TAB_COPIES

    def load(i):
        return pltpu.make_async_copy(
            table.at[pl.ds(i * part, part)], landed.at[i % 3], tab_sem.at[i]
        )

    def widen(i):
        load(i).wait()

        def body(n, _):
            at = pl.multiple_of(n * 48, 16)
            tab[pl.ds(pl.multiple_of(i * part + n * 48, 16), 48), :] = landed[
                i % 3, pl.ds(at, 48), :
            ].astype(F32)
            return 0

        lax.fori_loop(0, part // 48, body, 0)
        if i + 3 < TAB_COPIES:
            load(i + 3).start()

    for i in range(3):
        load(i).start()

    barrier = pltpu.get_barrier_semaphore()

    def greet_plane(i, _):
        dd = lax.rem(zl + i // 16, 2) * 4 + y
        tt = lax.rem(t + i, 16)
        pl.semaphore_signal(barrier, inc=1, device_id=(dd, tt), device_id_type=MESH)
        return 0

    lax.fori_loop(1, 32, greet_plane, 0)

    def greet_row(i, _):
        dd = lax.rem(zl + i // 3, 2) * 4 + lax.rem(y + 1 + lax.rem(i, 3), 4)
        pl.semaphore_signal(barrier, inc=1, device_id=(dd, t), device_id_type=MESH)
        return 0

    lax.fori_loop(0, 6, greet_row, 0)
    tab[pl.ds(ROWS, 8), :] = jnp.zeros((8, 512), F32)
    widen(0)
    pl.semaphore_wait(barrier, 37)

    for i in range(1, 8):
        send(ids.at[0], ids_all.at[d], ids_ss.at[i - 1], ids_rs.at[i - 1], (lax.rem(d + i, 8), t))

    row = pl.multiple_of(((zl * 2 + h) * 4 + lax.rem(x, 2) * 2 + k) * 64, 64)
    plane = x // 2

    def pieces(tt, wkv):
        q0 = pl.multiple_of(tt * 512, 256)
        c0 = pl.multiple_of((tt // 2) * HEAD, HEAD)
        return (
            (wkv.at[:, pl.ds(c0, HEAD)], wa.at[y, pl.ds(row, 64), pl.ds(0, HEAD)], 0),
            (wq.at[:, pl.ds(q0, 256)], wa.at[y, pl.ds(row, 64), pl.ds(HEAD, 256)], 0),
            (wq.at[:, pl.ds(pl.multiple_of(q0 + 256, 256), 256)], wb.at[y, pl.ds(row, 64), :], 1),
        )

    def outgoing(i, tt, wkv):
        return [
            pltpu.make_async_remote_copy(
                src_ref=src, dst_ref=dst, send_sem=x_ss.at[i, n], recv_sem=x_rs.at[r],
                device_id=(plane * 4 + y, tt), device_id_type=MESH,
            )
            for n, (src, dst, r) in enumerate(pieces(tt, wkv))
        ]

    def distribute(i, _):
        tt = lax.rem(t + i, 16)
        here = jnp.logical_and(i == 0, plane == zl)
        for core, wkv in ((0, wk), (1, wv)):
            turn = lax.rem(tt, 2) == core

            @pl.when(jnp.logical_and(turn, jnp.logical_not(here)))
            def _():
                for copy in outgoing(i, tt, wkv):
                    copy.start()

            @pl.when(jnp.logical_and(turn, here))
            def _():
                for src, dst, r in pieces(tt, wkv):
                    pltpu.make_async_copy(src, dst, x_rs.at[r]).start()

        return 0

    lax.fori_loop(0, 16, distribute, 0)

    for i in range(1, TAB_COPIES):
        widen(i)
    ids_all[d] = ids[0]
    for i in range(1, 8):
        arrived(ids_all.at[lax.rem(d + 8 - i, 8)], ids_ss.at[i - 1], ids_rs.at[i - 1])
    local = ids_all[...] - d * ROWS
    index_v[...] = jnp.where((local >= 0) & (local < ROWS), local, ROWS)
    to_scalar = pltpu.make_async_copy(index_v, index_s, sm_sem)
    to_scalar.start()
    to_scalar.wait()

    def gather(c, rel, g):
        group = g * 4 + lax.rem(y + rel, 4)

        def pick(i, _):
            line, first = c * 2 + i // 8, lax.rem(i, 8) * 16
            for j in range(16):
                stage[pl.ds(i * 16 + j, 1), :] = tab[pl.ds(index_s[group, line, first + j], 1), :]
            return 0

        lax.fori_loop(0, PART // 16, pick, 0)

        def narrow(i, _):
            rows = pl.ds(pl.multiple_of(i * 64, 64), 64)
            mine[c, rel, g, rows, :] = stage[rows, :].astype(BF16)
            return 0

        lax.fori_loop(0, PART // 64, narrow, 0)

    def first_sends(c):
        send(mine.at[c, 2, 0], half_in.at[c, 0], g_ss.at[c, 0], h_rs.at[c, 0], up)
        send(mine.at[c, 2, 1], half_in.at[c, 1], g_ss.at[c, 1], h_rs.at[c, 1], down)
        send(mine.at[c, 1, 1], final_in.at[c, 0, 1], g_ss.at[c, 2], f_rs.at[c, 0, 1], up)
        send(mine.at[c, 3, 0], final_in.at[c, 1, 0], g_ss.at[c, 3], f_rs.at[c, 1, 0], down)

    def second_sends(c):
        arrived(half_in.at[c, 0], g_ss.at[c, 0], h_rs.at[c, 0])
        mine[c, 1, 0] = mine[c, 1, 0] + half_in[c, 0]
        send(mine.at[c, 1, 0], final_in.at[c, 0, 0], g_ss.at[c, 4], f_rs.at[c, 0, 0], up)
        arrived(half_in.at[c, 1], g_ss.at[c, 1], h_rs.at[c, 1])
        mine[c, 3, 1] = mine[c, 3, 1] + half_in[c, 1]
        send(mine.at[c, 3, 1], final_in.at[c, 1, 1], g_ss.at[c, 5], f_rs.at[c, 1, 1], down)

    kept = pl.multiple_of(zl * 256, 256)
    given = pl.multiple_of((1 - zl) * 256, 256)

    def finish_rows(c):
        for g in range(2):
            for side in range(2):
                arrived(final_in.at[c, side, g], g_ss.at[c, 0], f_rs.at[c, side, g])
            rows = pl.ds(g * PART, PART)
            for at, to in ((given, None), (kept, t)):
                cols = pl.ds(at, 256)
                total = mine[c, 0, g, :, cols] + final_in[c, 0, g, :, cols] + final_in[c, 1, g, :, cols]
                if to is None:
                    zsend[c, rows, :] = total
                else:
                    acts[to, c, rows, :] = total
        send(zsend.at[c], zrecv.at[c], z_ss.at[c], z_rs.at[c], over)

    at_xp, at_xm = (d, slot(h, xp, k)), (d, slot(h, xm, k))
    at_z, at_core = (d, slot(1 - h, x, k)), (d, slot(h, x, 1 - k))

    def push(c, s, i, device):
        send(acts.at[s, c], acts.at[s, c], a_ss.at[c, i], a_rs.at[c, s], device)

    def have(c, s):
        arrived(acts.at[s, c], a_ss.at[c, 0], a_rs.at[c, s])

    def spread_own(c):
        arrived(zrecv.at[c], z_ss.at[c], z_rs.at[c])
        acts[t, c] = acts[t, c] + zrecv[c]
        push(c, t, 0, at_z)
        push(c, t, 1, at_xp)
        push(c, t, 2, at_xm)
        push(c, t, 3, at_core)

    def spread_near(c):
        s = slot(h, xm, k)
        have(c, s)
        push(c, s, 4, at_xp)
        push(c, s, 5, at_core)
        s = slot(h, xp, k)
        have(c, s)
        push(c, s, 6, at_core)

    def spread_far(c):
        s = slot(1 - h, x, k)
        have(c, s)
        push(c, s, 7, at_xp)
        push(c, s, 8, at_xm)
        push(c, s, 9, at_core)

    def spread_rest(c):
        s = slot(1 - h, xp, k)
        have(c, s)
        push(c, s, 10, at_xm)
        push(c, s, 11, at_core)
        s = slot(1 - h, xm, k)
        have(c, s)
        push(c, s, 12, at_core)
        for i in range(2):
            s = slot(i, x2, k)
            have(c, s)
            push(c, s, 13 + i, at_core)

    top, low = pl.ds(0, 512), pl.ds(512, 512)

    def pushw(ref, b, rows, i, rs, device):
        src = ref.at[b] if rows is None else ref.at[b, rows]
        send(src, src, w_ss.at[i], rs, device)

    def whole_weights(ref, r):
        pltpu.make_async_copy(ref.at[y], ref.at[y], x_rs.at[r]).wait()

    def first_weights():
        whole_weights(wa, 0)
        pushw(wa, y, None, 0, wa_rs.at[0], up)
        pushw(wa, y, None, 1, wa_rs.at[1], down)
        whole_weights(wb, 1)
        pushw(wb, y, top, 2, wb_rs.at[0], up)
        pushw(wb, y, low, 3, wb_rs.at[1], down)

    def relay_weights():
        arrived(wa.at[ym], w_ss.at[0], wa_rs.at[0])
        pushw(wa, ym, top, 4, wa_rs.at[2], up)
        arrived(wa.at[yp], w_ss.at[0], wa_rs.at[1])
        pushw(wa, yp, low, 5, wa_rs.at[3], down)
        pushw(wb, y, low, 6, wb_rs.at[4], up)
        pushw(wb, y, top, 7, wb_rs.at[5], down)

    def last_weights():
        arrived(wb.at[ym, top], w_ss.at[0], wb_rs.at[0])
        pushw(wb, ym, top, 8, wb_rs.at[2], up)
        arrived(wb.at[yp, low], w_ss.at[0], wb_rs.at[1])
        pushw(wb, yp, low, 9, wb_rs.at[3], down)

    def squares(c):
        for hh in range(2):
            for xx in range(4):
                have(c, slot(hh, xx, 1 - k))

        def body(i, _):
            rows = pl.ds(pl.multiple_of(i * 64, 64), 64)
            total = jnp.zeros((64, 128), F32)
            for s in range(16):
                v = acts[s, c, rows, :].astype(F32)
                v = v * v
                total = total + (v[:, :128] + v[:, 128:])
            sq[rows, :] = total
            return 0

        lax.fori_loop(0, 8, body, 0)
        for i in range(4):
            sq_own[c, i : i + 1, :] = jnp.sum(
                jnp.transpose(sq[i * 128 : (i + 1) * 128, :]), axis=0, keepdims=True
            )
        send(sq_own.at[c], sq_in.at[c], q_ss.at[c], q_rs.at[c], over)

    def norm(c):
        arrived(sq_in.at[c], q_ss.at[c], q_rs.at[c])
        for i in range(4):
            mean = (sq_own[c, i : i + 1, :] + sq_in[c, i : i + 1, :]) * (1.0 / 8192.0)
            inv[i * 128 : (i + 1) * 128, :] = jnp.transpose(
                jnp.broadcast_to(lax.rsqrt(mean + 1e-06), (128, 128))
            )

        def body(s, _):
            a, b, cc = s // 8, lax.rem(s // 2, 4), lax.rem(s, 2)
            at = pl.multiple_of(b * 1024 + (a * 2 + cc) * 256, 256)
            weight = gain[s * 2 + zl]
            for g in range(2):
                rows = pl.ds(g * PART, PART)
                scale = inv[rows, :]
                v = acts[s, c, rows, :].astype(F32)
                v = v * jnp.concatenate([scale, scale], axis=1) * weight
                normed[g, pl.ds(c * PART, PART), pl.ds(at, 256)] = v.astype(BF16)
            return 0

        lax.fori_loop(0, 16, body, 0)

    def project(g, w, acc, blocks, fresh):
        def body(i, _):
            b = lax.rem(y + blocks(i), 4)
            cols = pl.ds(pl.multiple_of(b * 1024, 1024), 1024)
            acc[...] += jnp.dot(normed[g, :, cols], w[b], preferred_element_type=F32)
            return 0

        if fresh:
            acc[...] = jnp.zeros_like(acc)
        lax.fori_loop(0, 4, body, 0)

    def rotate(v):
        return v * cosine[...] + pltpu.roll(v, 64, axis=1) * sine[...]

    def attend(query, head):
        for block in range(2):
            seen = (block + 1) * 256
            rows = slice(block * 256, seen)
            scores = lax.dot_general(
                query[rows], kv[0, :seen, :], (((1,), (1,)), ((), ())), preferred_element_type=F32
            ) * (1.0 / HEAD**0.5)
            i = lax.broadcasted_iota(I32, (256, seen), 0) + block * 256
            j = lax.broadcasted_iota(I32, (256, seen), 1)
            allowed = (j <= i) & (first_col[rows, :] == first_row[:, :seen])
            scores = jnp.where(allowed, scores, NEG)
            largest = jnp.max(scores, axis=-1, keepdims=True)
            weight = jnp.where(allowed, jnp.exp(scores - largest), 0.0)
            probs = (weight / jnp.sum(weight, axis=-1, keepdims=True)).astype(BF16)
            out[rows, head * HEAD : (head + 1) * HEAD] = jnp.dot(
                probs, kv[1, :seen, :], preferred_element_type=F32
            ).astype(BF16)

    gather(0, 2, 0)
    gather(0, 2, 1)
    gather(0, 1, 1)
    gather(0, 3, 0)
    first_sends(0)
    for rel, g in ((1, 0), (3, 1), (0, 0), (0, 1)):
        gather(0, rel, g)
    for rel, g in ((2, 0), (2, 1), (1, 1), (3, 0)):
        gather(1, rel, g)
    second_sends(0)
    first_sends(1)
    for rel, g in ((1, 0), (3, 1), (0, 0), (0, 1)):
        gather(1, rel, g)
    finish_rows(0)
    second_sends(1)
    spread_own(0)
    first_weights()
    finish_rows(1)
    spread_near(0)
    spread_far(0)
    spread_own(1)
    spread_rest(0)
    spread_near(1)
    relay_weights()
    spread_far(1)
    last_weights()
    squares(0)
    spread_rest(1)
    norm(0)
    squares(1)
    norm(1)

    own, other = zl, 1 - zl
    order = lambda i: i
    arrived(wa.at[y2, top], w_ss.at[0], wa_rs.at[2])
    arrived(wa.at[y2, low], w_ss.at[0], wa_rs.at[3])
    project(other, wa, acca, order, True)
    psa[...] = acca[...]
    send(psa, pra, p_ss.at[0], p_rs.at[0], over)
    project(own, wa, acca, order, True)
    arrived(pra, p_ss.at[0], p_rs.at[0])
    first = acca[:, 0:HEAD] + pra[:, 0:HEAD]
    kv[k] = jnp.where(k == 0, rotate(first), first).astype(BF16)
    send(kv.at[k], kv.at[k], kv_ss, kv_rs, at_core)
    arrived(kv.at[1 - k], kv_ss, kv_rs)
    for n in range(2):
        cols = slice((n + 1) * HEAD, (n + 2) * HEAD)
        attend(rotate(acca[:, cols] + pra[:, cols]).astype(BF16), n)

    arrived(wb.at[ym, low], w_ss.at[0], wb_rs.at[4])
    arrived(wb.at[yp, top], w_ss.at[0], wb_rs.at[5])
    arrived(wb.at[y2, top], w_ss.at[0], wb_rs.at[2])
    arrived(wb.at[y2, low], w_ss.at[0], wb_rs.at[3])
    project(other, wb, accb, order, True)
    psb[...] = accb[...]
    send(psb, prb, p_ss.at[1], p_rs.at[1], over)
    project(own, wb, accb, order, True)
    arrived(prb, p_ss.at[1], p_rs.at[1])
    for n in range(2):
        cols = slice(n * HEAD, (n + 1) * HEAD)
        attend(rotate(accb[:, cols] + prb[:, cols]).astype(BF16), 2 + n)

    for copy in started:
        copy.wait_send()

    def settle(i, _):
        tt = lax.rem(t + i, 16)

        @pl.when(jnp.logical_not(jnp.logical_and(i == 0, plane == zl)))
        def _():
            for copy in outgoing(i, tt, wk):
                copy.wait_send()

        return 0

    lax.fori_loop(0, 16, settle, 0)


def on_device(token_ids, positions, embed_table, norm_gain, wq, wk, wv):
    frequency = 1000000.0 ** (-(jnp.arange(64, dtype=F32) * 2.0 / HEAD))
    angles = positions.astype(F32)[:, None] * frequency[None, :]
    cosine, sine = jnp.cos(angles), jnp.sin(angles)
    first = jnp.arange(TOK, dtype=I32) - positions
    vmem = pl.BlockSpec(memory_space=pltpu.VMEM)
    far = pl.BlockSpec(memory_space=pl.ANY)
    dma = pltpu.SemaphoreType.DMA
    return pl.pallas_call(
        kernel,
        out_shape=jax.ShapeDtypeStruct((TOK, 512), BF16),
        in_specs=[vmem] * 6 + [far] * 4,
        out_specs=vmem,
        scratch_shapes=[
            pltpu.VMEM((3, ROWS // TAB_COPIES, 512), BF16),
            pltpu.VMEM((ROWS + 8, 512), F32),
            pltpu.VMEM((PART, 512), F32),
            pltpu.VMEM((8, 4, 128), I32),
            pltpu.VMEM((8, 4, 128), I32),
            pltpu.SMEM((8, 4, 128), I32),
            pltpu.VMEM((2, 4, 2, PART, 512), BF16),
            pltpu.VMEM((2, 2, PART, 512), BF16),
            pltpu.VMEM((2, 2, 2, PART, 512), BF16),
            pltpu.VMEM((2, 512, 256), BF16),
            pltpu.VMEM((2, 512, 256), BF16),
            pltpu.VMEM((16, 2, 512, 256), BF16),
            pltpu.VMEM((2, 512, 4096), BF16),
            pltpu.VMEM((4, 1024, 384), BF16),
            pltpu.VMEM((4, 1024, 256), BF16),
            pltpu.VMEM((TOK, 384), F32),
            pltpu.VMEM((TOK, 384), F32),
            pltpu.VMEM((TOK, 256), F32),
            pltpu.VMEM((TOK, 256), F32),
            pltpu.VMEM((TOK, 384), F32),
            pltpu.VMEM((TOK, 256), F32),
            pltpu.VMEM((2, TOK, HEAD), BF16),
            pltpu.VMEM((512, 128), F32),
            pltpu.VMEM((2, 4, 128), F32),
            pltpu.VMEM((2, 4, 128), F32),
            pltpu.VMEM((512, 128), F32),
            dma((7,)), dma((7,)), dma((TAB_COPIES,)), dma,
            dma((16, 3)), dma((2,)),
            dma((2, 6)), dma((2, 2)), dma((2, 2, 2)),
            dma((2,)), dma((2,)),
            dma((2, 15)), dma((2, 16)),
            dma((2,)), dma((2,)),
            dma((10,)), dma((4,)), dma((6,)),
            dma((2,)), dma((2,)),
            dma, dma,
        ],
        compiler_params=pltpu.CompilerParams(
            collective_id=0, has_side_effects=True, vmem_limit_bytes=63 * 2**20
        ),
    )(
        token_ids.reshape(1, 4, 128),
        jnp.concatenate([cosine, cosine], axis=1),
        jnp.concatenate([-sine, sine], axis=1),
        first.reshape(TOK, 1),
        first.reshape(1, TOK),
        norm_gain.reshape(32, 1, 256),
        embed_table,
        wq,
        wk,
        wv,
    )


def solution(mesh):
    split = P(("dp", "tensor"), None)
    return jax.shard_map(
        on_device,
        mesh=mesh,
        in_specs=(P("dp"), P("dp"), P("dp", "tensor"), P(), split, split, split),
        out_specs=P("dp", "tensor"),
        check_vma=False,
    )
```

time: 345 us -> 146 us (0.42)
  waiting for transfers between devices: 221 us -> 0 us
  Pallas kernels: 0 us -> 138 us
  local copies, waits for them, and re-layouts: 41.9 us -> 2.72 us
  blocking collectives: 31.3 us -> 0 us
  other arithmetic: 17.8 us -> 2.75 us
  between operations: 14.8 us -> 0.02 us
  matrix products: 11.1 us -> 0 us
  starting transfers between devices: 5.23 us -> 0 us
    reduce_scatter x1 -> x0, waiting for transfers between devices: 145 us -> none  [on_device(): lax.psum_scatter(partial_value, DP, scatter_dimension=0, tiled=True)]
    pallas_call x0 -> x1, Pallas kernels: none -> 138 us  [on_device(): pl.pallas_call(kernel, out_shape=jax.ShapeDtypeStruct((TOK, 512), BF16),...]
    all_gather x3 -> x0, waiting for transfers between devices: 69.4 us -> none  [the longest x1 64.4 us: on_device(): features = lax.all_gather(embedded, 'tensor', axis=1, tiled=True)]
    all_to_all x1 -> x0, blocking collectives: 31.3 us -> none  [on_device(): lax.all_to_all(combined, 'tensor', split_axis=1, concat_axis=0, tiled=True)]
    gather x1 -> x0, local copies, waits for them, and re-layouts: 22.4 us -> none  [on_device(): jnp.take(embed_table, jnp.clip(local_ids, 0, vocab_rows - 1), axis=0)]
    dot_general x3 -> x0, matrix products: 11.1 us -> none  [the longest x1 9.86 us: on_device(): jnp.dot(normed_hidden, whole_of(owner_rows, DP, (0, 1), 0), preferred_ele...]
    transpose x1 -> x0, local copies, waits for them, and re-layouts: 10.8 us -> none  [gather_in_order(): pieces.transpose(*turned, *range(len(sequence), pieces.ndim))]
    all_to_all x1 -> x0, waiting for transfers between devices: 6.16 us -> none  [from_everyone(): lax.all_to_all(jnp.broadcast_to(x[None], (count, *x.shape)), axis, 0, 0,...]
  transfers between devices with their start and end apart: 5 -> 0, of which waited for: 4 -> 0; matrix products, arithmetic and copies ran while one was open for 12% -> 0% of each run, Pallas kernels for 0% -> 0%
where the time goes in v1:
time: 146 us; the launch traced here: 144 us
  Pallas kernels  138 us (95%)
  other arithmetic  2.75 us (2%)
  local copies, waits for them, and re-layouts  2.72 us (2%)
    pallas_call x1, Pallas kernels, on_device(): pl.pallas_call(kernel, out_shape=jax.ShapeDtypeStruct((TOK, 512), BF16),...  138 us

profile of v1, /device:TPU:0, one launch (start us, length us, event | category | flops | bytes accessed | tf_op | source)
XLA Modules:
  0.0 143.7 jit_solution(7340529758715495022)
XLA Ops:
  0.0 0.8 iota_subtract_fusion
  0.8 0.0 copy-start
  0.8 1.0 fusion
  1.8 1.0 pad_maximum_fusion
  2.8 0.9 copy.8.first_col
  3.6 0.0 copy-done
  3.6 138.2 %shard_map.73 = bf16[512,512]{1,0:T(8,128)(2,1)} custom-call(s32[1,4,128]{2,1,0:T(4,128)} %bitcast.7, f32[512,128]{1,0:T(8,128)} %get-tuple-element.10.cosine, f32[512,128]{1,0:T(8,128)} %get-tuple-element.11.sine, s32[512,1]{1,0:T(8,128)} %copy.8.first_col, s32[1,512]{1,0:T(1,128)} %bitcast.6, f32[32,1,256]{2,1,0:T(1,128)} %bitcast.4, ...), custom_call_target="tpu_custom_call" | custom-call | tf_op jit(solution)/shard_map/pallas_call | solution.py:438
  141.8 1.9 %copy.10 = bf16[512,512]{1,0:T(8,128)(2,1)} copy(bf16[512,512]{1,0:T(8,128)(2,1)} %shard_map.73) | data formatting | bytes 1048576
  (1 shorter events, 0.0 us)
Async XLA Ops:
  0.8 2.9 %copy-start = (s32[512]{0:T(512)}, s32[512]{0:T(512)S(1)}, u32[]{:S(2)}) copy-start(s32[512]{0:T(512)S(1)} %get-tuple-element.8) | copy-start | bytes 6148

commit v2 on v1

v2 whole, which is shorter than its diff:
```python
import jax
import jax.numpy as jnp
from jax import lax
from jax.experimental import pallas as pl
from jax.experimental.pallas import tpu as pltpu
from jax.sharding import PartitionSpec as P

MESH = pl.DeviceIdType.MESH
F32, BF16, I32 = jnp.float32, jnp.bfloat16, jnp.int32
TOK = 512
PART = 128
CHUNKS = TOK // PART
SPLIT = 2
BAND = TOK // SPLIT
PIECES = 5
ROWS = 9504
HEAD = 128
TAB_COPIES = 6
NEG = -1e30


def kernel(
    ids, place, frequency, gain, table, wq, wk, wv, out,
    landed, tab, stage, ids_all, index_v, index_s, mine, half_in, final_in,
    zsend, zrecv, acts, normed, weights, psend, precv, kept_sum, kv,
    sq, sq_own, sq_in, inv, cosine, sine, first_col,
    ids_ss, ids_rs, tab_sem, sm_sem, x_ss, x_rs, g_ss, h_rs, f_rs, z_ss, z_rs,
    a_ss, a_rs, q_ss, q_rs, w_ss, w_rs, p_ss, p_rs, kv_ss, kv_rs,
):
    d = lax.axis_index("dp")
    t = lax.axis_index("tensor")
    zl, y = d // 4, lax.rem(d, 4)
    h, x, k = t // 8, lax.rem(t // 2, 4), lax.rem(t, 2)
    yp, y2, ym = lax.rem(y + 1, 4), lax.rem(y + 2, 4), lax.rem(y + 3, 4)
    xp, x2, xm = lax.rem(x + 1, 4), lax.rem(x + 2, 4), lax.rem(x + 3, 4)
    up, down, over = (zl * 4 + yp, t), (zl * 4 + ym, t), ((1 - zl) * 4 + y, t)

    def slot(hh, xx, kk):
        return hh * 8 + xx * 2 + kk

    started = []

    def send(src, dst, ss, rs, device):
        copy = pltpu.make_async_remote_copy(
            src_ref=src, dst_ref=dst, send_sem=ss, recv_sem=rs, device_id=device, device_id_type=MESH
        )
        copy.start()
        started.append(copy)

    def arrived(dst, ss, rs):
        pltpu.make_async_remote_copy(
            src_ref=dst, dst_ref=dst, send_sem=ss, recv_sem=rs, device_id=over, device_id_type=MESH
        ).wait_recv()

    part = ROWS // TAB_COPIES

    def load(i):
        return pltpu.make_async_copy(
            table.at[pl.ds(i * part, part)], landed.at[i % 3], tab_sem.at[i]
        )

    def widen(i):
        load(i).wait()

        def body(n, _):
            at = pl.multiple_of(n * 48, 16)
            tab[pl.ds(pl.multiple_of(i * part + n * 48, 16), 48), :] = landed[
                i % 3, pl.ds(at, 48), :
            ].astype(F32)
            return 0

        lax.fori_loop(0, part // 48, body, 0)
        if i + 3 < TAB_COPIES:
            load(i + 3).start()

    for i in range(3):
        load(i).start()

    barrier = pltpu.get_barrier_semaphore()

    def greet_plane(i, _):
        dd = lax.rem(zl + i // 16, 2) * 4 + y
        tt = lax.rem(t + i, 16)
        pl.semaphore_signal(barrier, inc=1, device_id=(dd, tt), device_id_type=MESH)
        return 0

    lax.fori_loop(1, 32, greet_plane, 0)

    def greet_row(i, _):
        dd = lax.rem(zl + i // 3, 2) * 4 + lax.rem(y + 1 + lax.rem(i, 3), 4)
        pl.semaphore_signal(barrier, inc=1, device_id=(dd, t), device_id_type=MESH)
        return 0

    lax.fori_loop(0, 6, greet_row, 0)
    pl.semaphore_wait(barrier, 37)

    for i in range(1, 8):
        send(ids.at[0], ids_all.at[d], ids_ss.at[i - 1], ids_rs.at[i - 1], (lax.rem(d + i, 8), t))

    tab[pl.ds(ROWS, 8), :] = jnp.zeros((8, 512), F32)
    for i in range(TAB_COPIES):
        widen(i)

    row = pl.multiple_of(((zl * 2 + h) * 4 + lax.rem(x, 2) * 2 + k) * 64, 64)
    plane = x // 2

    def pieces(tt, wkv):
        q0 = pl.multiple_of(tt * 512, 256)
        c0 = pl.multiple_of((tt // 2) * HEAD, HEAD)
        to = [weights.at[j, y, pl.ds(row, 64), :] for j in range(PIECES)]
        return [(wkv.at[:, pl.ds(c0, HEAD)], to[0], 0)] + [
            (wq.at[:, pl.ds(pl.multiple_of(q0 + n * HEAD, HEAD), HEAD)], to[n + 1], n + 1)
            for n in range(4)
        ]

    def outgoing(i, tt, wkv):
        return [
            pltpu.make_async_remote_copy(
                src_ref=src, dst_ref=dst, send_sem=x_ss.at[i, n], recv_sem=x_rs.at[r],
                device_id=(plane * 4 + y, tt), device_id_type=MESH,
            )
            for n, (src, dst, r) in enumerate(pieces(tt, wkv))
        ]

    def distribute(i, _):
        tt = lax.rem(t + i, 16)
        here = jnp.logical_and(i == 0, plane == zl)
        for core, wkv in ((0, wk), (1, wv)):
            turn = lax.rem(tt, 2) == core

            @pl.when(jnp.logical_and(turn, jnp.logical_not(here)))
            def _():
                for copy in outgoing(i, tt, wkv):
                    copy.start()

            @pl.when(jnp.logical_and(turn, here))
            def _():
                for src, dst, r in pieces(tt, wkv):
                    pltpu.make_async_copy(src, dst, x_rs.at[r]).start()

        return 0

    def distribute_all():
        lax.fori_loop(0, 16, distribute, 0)

    ids_all[d] = ids[0]
    for i in range(1, 8):
        arrived(ids_all.at[lax.rem(d + 8 - i, 8)], ids_ss.at[i - 1], ids_rs.at[i - 1])
    local = ids_all[...] - d * ROWS
    index_v[...] = jnp.where((local >= 0) & (local < ROWS), local, ROWS)
    to_scalar = pltpu.make_async_copy(index_v, index_s, sm_sem)
    to_scalar.start()
    to_scalar.wait()

    def gather(c, rel, g):
        group = g * 4 + lax.rem(y + rel, 4)

        def pick(i, _):
            for j in range(16):
                stage[pl.ds(i * 16 + j, 1), :] = tab[pl.ds(index_s[group, c, i * 16 + j], 1), :]
            return 0

        lax.fori_loop(0, PART // 16, pick, 0)

        def narrow(i, _):
            rows = pl.ds(pl.multiple_of(i * 64, 64), 64)
            mine[c, rel, g, rows, :] = stage[rows, :].astype(BF16)
            return 0

        lax.fori_loop(0, PART // 64, narrow, 0)

    def rows_a(c):
        for g, to in ((0, up), (1, down)):
            gather(c, 2, g)
            send(mine.at[c, 2, g], half_in.at[c, g], g_ss.at[c, g], h_rs.at[c, g], to)

    def rows_b(c):
        gather(c, 1, 1)
        send(mine.at[c, 1, 1], final_in.at[c, 0, 1], g_ss.at[c, 2], f_rs.at[c, 0, 1], up)
        gather(c, 3, 0)
        send(mine.at[c, 3, 0], final_in.at[c, 1, 0], g_ss.at[c, 3], f_rs.at[c, 1, 0], down)

    def rows_own(c):
        for rel, g in ((1, 0), (3, 1), (0, 0), (0, 1)):
            gather(c, rel, g)

    def rows_c(c):
        arrived(half_in.at[c, 0], g_ss.at[c, 0], h_rs.at[c, 0])
        mine[c, 1, 0] = mine[c, 1, 0] + half_in[c, 0]
        send(mine.at[c, 1, 0], final_in.at[c, 0, 0], g_ss.at[c, 4], f_rs.at[c, 0, 0], up)
        arrived(half_in.at[c, 1], g_ss.at[c, 1], h_rs.at[c, 1])
        mine[c, 3, 1] = mine[c, 3, 1] + half_in[c, 1]
        send(mine.at[c, 3, 1], final_in.at[c, 1, 1], g_ss.at[c, 5], f_rs.at[c, 1, 1], down)

    kept = pl.multiple_of(zl * 256, 256)
    given = pl.multiple_of((1 - zl) * 256, 256)

    def finish_rows(c):
        for g in range(2):
            for side in range(2):
                arrived(final_in.at[c, side, g], g_ss.at[c, 0], f_rs.at[c, side, g])
            rows = pl.ds(g * PART, PART)
            for at, to in ((given, None), (kept, t)):
                cols = pl.ds(at, 256)
                total = mine[c, 0, g, :, cols] + final_in[c, 0, g, :, cols] + final_in[c, 1, g, :, cols]
                if to is None:
                    zsend[c, rows, :] = total
                else:
                    acts[to, c, rows, :] = total
        send(zsend.at[c], zrecv.at[c], z_ss.at[c], z_rs.at[c], over)

    at_xp, at_xm = (d, slot(h, xp, k)), (d, slot(h, xm, k))
    at_z, at_core = (d, slot(1 - h, x, k)), (d, slot(h, x, 1 - k))

    def push(c, s, i, device):
        send(acts.at[s, c], acts.at[s, c], a_ss.at[c, i], a_rs.at[c, s], device)

    def have(c, s):
        arrived(acts.at[s, c], a_ss.at[c, 0], a_rs.at[c, s])

    def spread_own(c):
        arrived(zrecv.at[c], z_ss.at[c], z_rs.at[c])
        acts[t, c] = acts[t, c] + zrecv[c]
        push(c, t, 0, at_z)
        push(c, t, 1, at_xp)
        push(c, t, 2, at_xm)
        push(c, t, 3, at_core)

    def spread_near(c):
        s = slot(h, xm, k)
        have(c, s)
        push(c, s, 4, at_xp)
        push(c, s, 5, at_core)

    def spread_far(c):
        s = slot(1 - h, x, k)
        have(c, s)
        push(c, s, 7, at_xm)
        push(c, s, 8, at_xp)
        push(c, s, 9, at_core)

    def spread_pass(c):
        s = slot(1 - h, xp, k)
        have(c, s)
        push(c, s, 10, at_xm)
        push(c, s, 11, at_core)

    def spread_rest(c):
        for i, s in (
            (6, slot(h, xp, k)), (12, slot(1 - h, xm, k)), (13, slot(0, x2, k)), (14, slot(1, x2, k)),
        ):
            have(c, s)
            push(c, s, i, at_core)

    top, low = pl.ds(0, 512), pl.ds(512, 512)

    def weights_own(j):
        src = weights.at[j, y]
        pltpu.make_async_copy(src, src, x_rs.at[j]).wait()
        send(src, src, w_ss.at[j, 0], w_rs.at[j, 0], up)
        send(src, src, w_ss.at[j, 1], w_rs.at[j, 1], down)

    def weights_pass(j):
        arrived(weights.at[j, ym], w_ss.at[j, 0], w_rs.at[j, 0])
        src = weights.at[j, ym, top]
        send(src, src, w_ss.at[j, 2], w_rs.at[j, 2], up)
        arrived(weights.at[j, yp], w_ss.at[j, 0], w_rs.at[j, 1])
        src = weights.at[j, yp, low]
        send(src, src, w_ss.at[j, 3], w_rs.at[j, 3], down)

    def weights_whole(j):
        arrived(weights.at[j, y2, top], w_ss.at[j, 0], w_rs.at[j, 2])
        arrived(weights.at[j, y2, low], w_ss.at[j, 0], w_rs.at[j, 3])

    def squares(c):
        for hh in range(2):
            for xx in range(4):
                have(c, slot(hh, xx, 1 - k))

        def body(i, _):
            rows = pl.ds(pl.multiple_of(i * 64, 64), 64)
            total = jnp.zeros((64, 128), F32)
            for s in range(16):
                v = acts[s, c, rows, :].astype(F32)
                v = v * v
                total = total + (v[:, :128] + v[:, 128:])
            sq[rows, :] = total
            return 0

        lax.fori_loop(0, 4, body, 0)
        for i in range(2):
            sq_own[c, i : i + 1, :] = jnp.sum(
                jnp.transpose(sq[i * 128 : (i + 1) * 128, :]), axis=0, keepdims=True
            )
        send(sq_own.at[c], sq_in.at[c], q_ss.at[c], q_rs.at[c], over)

    def norm(c):
        arrived(sq_in.at[c], q_ss.at[c], q_rs.at[c])
        for i in range(2):
            mean = (sq_own[c, i : i + 1, :] + sq_in[c, i : i + 1, :]) * (1.0 / 8192.0)
            inv[i * 128 : (i + 1) * 128, :] = jnp.transpose(
                jnp.broadcast_to(lax.rsqrt(mean + 1e-06), (128, 128))
            )

        def body(s, _):
            a, b, cc = s // 8, lax.rem(s // 2, 4), lax.rem(s, 2)
            at = pl.multiple_of(b * 1024 + (a * 2 + cc) * 256, 256)
            weight = gain[s * 2 + zl]
            for g in range(2):
                rows = pl.ds(g * PART, PART)
                scale = inv[rows, :]
                v = acts[s, c, rows, :].astype(F32)
                v = v * jnp.concatenate([scale, scale], axis=1) * weight
                normed[g, pl.ds(c * PART, PART), pl.ds(at, 256)] = v.astype(BF16)
            return 0

        lax.fori_loop(0, 16, body, 0)

    def project(g, j, first, count, out_ref):
        rows = pl.ds(first, count)

        def body(b, total):
            cols = pl.ds(pl.multiple_of(b * 1024, 1024), 1024)
            return total + jnp.dot(
                normed[g, rows, cols], weights[j, b], preferred_element_type=F32
            )

        out_ref[...] = lax.fori_loop(0, 4, body, jnp.zeros((count, HEAD), F32))

    own, other = zl, 1 - zl

    def give(j, n):
        project(other, j, n * BAND, BAND, psend.at[j, n])
        send(psend.at[j, n], precv.at[j, n], p_ss.at[j, n], p_rs.at[j, n], over)

    def keep(j):
        for n in range(2):
            project(own, j, n * 256, 256, kept_sum.at[j, pl.ds(n * 256, 256)])

    def result(j):
        for n in range(SPLIT):
            arrived(precv.at[j, n], p_ss.at[j, n], p_rs.at[j, n])
        return kept_sum[j] + precv[j].reshape(TOK, HEAD)

    def angles():
        for i in range(4):
            rows = slice(i * 128, (i + 1) * 128)
            at = jnp.transpose(jnp.broadcast_to(place[0, i : i + 1, :].astype(F32), (128, 128)))
            angle = at * frequency[...]
            lane = lax.broadcasted_iota(I32, (128, 128), 1)
            cosine[rows, :] = jnp.cos(angle)
            sine[rows, :] = jnp.where(lane < 64, -jnp.sin(angle), jnp.sin(angle))
            first_col[rows, :] = (
                lax.broadcasted_iota(I32, (128, 128), 0) + i * 128 - at.astype(I32)
            )

    def rotate(v):
        return v * cosine[...] + pltpu.roll(v, 64, axis=1) * sine[...]

    def first_row(n):
        return lax.broadcasted_iota(I32, (1, 128), 1) + n * 128 - place[0, n : n + 1, :]

    def attend(query, head):
        for block in range(2):
            seen = (block + 1) * 256
            rows = slice(block * 256, seen)
            scores = lax.dot_general(
                query[rows], kv[0, :seen, :], (((1,), (1,)), ((), ())), preferred_element_type=F32
            ) * (1.0 / HEAD**0.5)
            i = lax.broadcasted_iota(I32, (256, seen), 0) + block * 256
            j = lax.broadcasted_iota(I32, (256, seen), 1)
            starts = jnp.concatenate([first_col[rows, :]] * (seen // 128), axis=1)
            key_starts = jnp.concatenate([first_row(n) for n in range(seen // 128)], axis=1)
            allowed = (j <= i) & (starts == key_starts)
            scores = jnp.where(allowed, scores, NEG)
            largest = jnp.max(scores, axis=-1, keepdims=True)
            weight = jnp.where(allowed, jnp.exp(scores - largest), 0.0)
            probs = (weight / jnp.sum(weight, axis=-1, keepdims=True)).astype(BF16)
            out[rows, head * HEAD : (head + 1) * HEAD] = jnp.dot(
                probs, kv[1, :seen, :], preferred_element_type=F32
            ).astype(BF16)

    def keys():
        first = result(0)
        kv[k] = jnp.where(k == 0, rotate(first), first).astype(BF16)
        send(kv.at[k], kv.at[k], kv_ss, kv_rs, at_core)

    rows_a(0)
    rows_b(0)
    distribute_all()
    rows_a(1)
    rows_b(1)
    rows_own(0)
    rows_c(0)
    rows_own(1)
    rows_a(2)
    rows_own(2)
    rows_c(1)
    rows_b(2)
    finish_rows(0)
    rows_a(3)
    rows_own(3)
    rows_c(2)
    spread_own(0)
    finish_rows(1)
    rows_b(3)
    spread_near(0)
    spread_own(1)
    rows_c(3)
    angles()
    finish_rows(2)
    spread_far(0)
    weights_own(0)
    spread_near(1)
    weights_own(1)
    finish_rows(3)
    spread_pass(0)
    spread_own(2)
    spread_far(1)
    spread_own(3)
    weights_pass(0)
    spread_rest(0)
    spread_near(2)
    weights_own(2)
    squares(0)
    spread_far(2)
    spread_pass(1)
    weights_pass(1)
    norm(0)
    spread_near(3)
    spread_far(3)
    weights_own(3)
    spread_pass(2)
    spread_rest(1)
    weights_pass(2)
    spread_pass(3)
    squares(1)
    weights_own(4)
    spread_rest(2)
    norm(1)
    weights_whole(0)
    give(0, 0)
    weights_whole(1)
    give(1, 0)
    weights_pass(3)
    spread_rest(3)
    squares(2)
    weights_whole(2)
    give(2, 0)
    squares(3)
    norm(2)
    norm(3)
    give(0, 1)
    weights_pass(4)
    give(1, 1)
    give(2, 1)
    keep(0)
    weights_whole(3)
    give(3, 0)
    give(3, 1)
    keep(1)
    weights_whole(4)
    give(4, 0)
    give(4, 1)
    keys()
    keep(2)
    keep(3)
    keep(4)
    arrived(kv.at[1 - k], kv_ss, kv_rs)
    attend(rotate(result(1)).astype(BF16), 0)
    attend(rotate(result(2)).astype(BF16), 1)
    attend(rotate(result(3)).astype(BF16), 2)
    attend(rotate(result(4)).astype(BF16), 3)

    for copy in started:
        copy.wait_send()

    def settle(i, _):
        tt = lax.rem(t + i, 16)

        @pl.when(jnp.logical_not(jnp.logical_and(i == 0, plane == zl)))
        def _():
            for copy in outgoing(i, tt, wk):
                copy.wait_send()

        return 0

    lax.fori_loop(0, 16, settle, 0)


def on_device(token_ids, positions, embed_table, norm_gain, wq, wk, wv):
    frequency = 1000000.0 ** (-(jnp.arange(64, dtype=F32) * 2.0 / HEAD))
    vmem = pl.BlockSpec(memory_space=pltpu.VMEM)
    far = pl.BlockSpec(memory_space=pl.ANY)
    dma = pltpu.SemaphoreType.DMA
    return pl.pallas_call(
        kernel,
        out_shape=jax.ShapeDtypeStruct((TOK, 512), BF16),
        in_specs=[vmem] * 4 + [far] * 4,
        out_specs=vmem,
        scratch_shapes=[
            pltpu.VMEM((3, ROWS // TAB_COPIES, 512), BF16),
            pltpu.VMEM((ROWS + 8, 512), F32),
            pltpu.VMEM((PART, 512), F32),
            pltpu.VMEM((8, 4, 128), I32),
            pltpu.VMEM((8, 4, 128), I32),
            pltpu.SMEM((8, 4, 128), I32),
            pltpu.VMEM((CHUNKS, 4, 2, PART, 512), BF16),
            pltpu.VMEM((CHUNKS, 2, PART, 512), BF16),
            pltpu.VMEM((CHUNKS, 2, 2, PART, 512), BF16),
            pltpu.VMEM((CHUNKS, 2 * PART, 256), BF16),
            pltpu.VMEM((CHUNKS, 2 * PART, 256), BF16),
            pltpu.VMEM((16, CHUNKS, 2 * PART, 256), BF16),
            pltpu.VMEM((2, TOK, 4096), BF16),
            pltpu.VMEM((PIECES, 4, 1024, HEAD), BF16),
            pltpu.VMEM((PIECES, SPLIT, BAND, HEAD), F32),
            pltpu.VMEM((PIECES, SPLIT, BAND, HEAD), F32),
            pltpu.VMEM((PIECES, TOK, HEAD), F32),
            pltpu.VMEM((2, TOK, HEAD), BF16),
            pltpu.VMEM((2 * PART, 128), F32),
            pltpu.VMEM((CHUNKS, 2, 128), F32),
            pltpu.VMEM((CHUNKS, 2, 128), F32),
            pltpu.VMEM((2 * PART, 128), F32),
            pltpu.VMEM((TOK, 128), F32),
            pltpu.VMEM((TOK, 128), F32),
            pltpu.VMEM((TOK, 128), I32),
            dma((7,)), dma((7,)), dma((TAB_COPIES,)), dma,
            dma((16, PIECES)), dma((PIECES,)),
            dma((CHUNKS, 6)), dma((CHUNKS, 2)), dma((CHUNKS, 2, 2)),
            dma((CHUNKS,)), dma((CHUNKS,)),
            dma((CHUNKS, 15)), dma((CHUNKS, 16)),
            dma((CHUNKS,)), dma((CHUNKS,)),
            dma((PIECES, 4)), dma((PIECES, 4)),
            dma((PIECES, SPLIT)), dma((PIECES, SPLIT)),
            dma, dma,
        ],
        compiler_params=pltpu.CompilerParams(
            collective_id=0, has_side_effects=True, vmem_limit_bytes=63 * 2**20
        ),
    )(
        token_ids.reshape(1, 4, 128),
        positions.reshape(1, 4, 128),
        jnp.concatenate([frequency, frequency]).reshape(1, HEAD),
        norm_gain.reshape(32, 1, 256),
        embed_table,
        wq,
        wk,
        wv,
    )


def solution(mesh):
    split = P(("dp", "tensor"), None)
    return jax.shard_map(
        on_device,
        mesh=mesh,
        in_specs=(P("dp"), P("dp"), P("dp", "tensor"), P(), split, split, split),
        out_specs=P("dp", "tensor"),
        check_vma=False,
    )
```

time: 146 us -> 120 us (0.82); the launches traced: 144 us -> 119 us
  Pallas kernels: 138 us -> 117 us
  other arithmetic: 2.75 us -> 0.6 us
    pallas_call x1, Pallas kernels: 138 us -> 117 us  [on_device(): pl.pallas_call(kernel, out_shape=jax.ShapeDtypeStruct((TOK, 512), BF16),...]
where the time goes in v2:
time: 120 us; the launch traced here: 119 us
  Pallas kernels  117 us (98%)
  local copies, waits for them, and re-layouts  1.87 us (2%)
    pallas_call x1, Pallas kernels, on_device(): pl.pallas_call(kernel, out_shape=jax.ShapeDtypeStruct((TOK, 512), BF16),...  117 us

profile of v2, /device:TPU:0, one launch (start us, length us, event | category | flops | bytes accessed | tf_op | source)
XLA Modules:
  0.0 119.3 jit_solution(6813350630733432897)
XLA Ops:
  0.0 0.6 maximum_bitcast_fusion.frequency
  0.6 116.8 %shard_map.73 = bf16[512,512]{1,0:T(8,128)(2,1)} custom-call(s32[1,4,128]{2,1,0:T(4,128)} %bitcast.6, s32[1,4,128]{2,1,0:T(4,128)} %bitcast.7, f32[1,128]{1,0:T(1,128)} %maximum_bitcast_fusion.frequency, f32[32,1,256]{2,1,0:T(1,128)} %bitcast.5, bf16[9504,512]{1,0:T(8,128)(2,1)} %table.1, bf16[64,8192]{1,0:T(8,128)(2,1)} %wq.1, bf16[64,1024]{1,0:T(8,128)(2,1)} %wk.1, ...), custom_call_target="tpu_custom_call" | custom-call | tf_op jit(solution)/shard_map/pallas_call | solution.py:496
  117.4 1.9 %copy.9 = bf16[512,512]{1,0:T(8,128)(2,1)} copy(bf16[512,512]{1,0:T(8,128)(2,1)} %shard_map.73) | data formatting | bytes 1048576
  (1 shorter events, 0.0 us)

commit v3 on v2

--- a/solution.py
+++ b/solution.py
@@ -23,7 +23,7 @@
     ids, place, frequency, gain, table, wq, wk, wv, out,
     landed, tab, stage, ids_all, index_v, index_s, mine, half_in, final_in,
     zsend, zrecv, acts, normed, weights, psend, precv, kept_sum, kv,
-    sq, sq_own, sq_in, inv, cosine, sine, first_col,
+    sq, sq_own, sq_in, inv, cosine, sine, bias,
     ids_ss, ids_rs, tab_sem, sm_sem, x_ss, x_rs, g_ss, h_rs, f_rs, z_ss, z_rs,
     a_ss, a_rs, q_ss, q_rs, w_ss, w_rs, p_ss, p_rs, kv_ss, kv_rs,
 ):
@@ -320,12 +320,11 @@
         rows = pl.ds(first, count)
 
         def body(b, total):
-            cols = pl.ds(pl.multiple_of(b * 1024, 1024), 1024)
-            return total + jnp.dot(
-                normed[g, rows, cols], weights[j, b], preferred_element_type=F32
-            )
-
-        out_ref[...] = lax.fori_loop(0, 4, body, jnp.zeros((count, HEAD), F32))
+            cols = pl.ds(pl.multiple_of(b * 2048, 2048), 2048)
+            w = weights[j, pl.ds(b * 2, 2)].reshape(2048, HEAD)
+            return total + jnp.dot(normed[g, rows, cols], w, preferred_element_type=F32)
+
+        out_ref[...] = lax.fori_loop(0, 2, body, jnp.zeros((count, HEAD), F32))
 
     own, other = zl, 1 - zl
 
@@ -333,9 +332,8 @@
         project(other, j, n * BAND, BAND, psend.at[j, n])
         send(psend.at[j, n], precv.at[j, n], p_ss.at[j, n], p_rs.at[j, n], over)
 
-    def keep(j):
-        for n in range(2):
-            project(own, j, n * 256, 256, kept_sum.at[j, pl.ds(n * 256, 256)])
+    def keep(j, n):
+        project(own, j, n * 256, 256, kept_sum.at[j, pl.ds(n * 256, 256)])
 
     def result(j):
         for n in range(SPLIT):
@@ -350,15 +348,17 @@
             lane = lax.broadcasted_iota(I32, (128, 128), 1)
             cosine[rows, :] = jnp.cos(angle)
             sine[rows, :] = jnp.where(lane < 64, -jnp.sin(angle), jnp.sin(angle))
-            first_col[rows, :] = (
-                lax.broadcasted_iota(I32, (128, 128), 0) + i * 128 - at.astype(I32)
-            )
+            row = lax.broadcasted_iota(I32, (128, 128), 0) + i * 128
+            start = row - at.astype(I32)
+            for n in range(i + 1):
+                key = lane + n * 128
+                seen = (key <= row) & (start == key - place[0, n : n + 1, :])
+                bias[rows, n * 128 : (n + 1) * 128] = jnp.where(seen, 0.0, NEG)
+            if i % 2 == 0:
+                bias[rows, (i + 1) * 128 : (i + 2) * 128] = jnp.full((128, 128), NEG, F32)
 
     def rotate(v):
         return v * cosine[...] + pltpu.roll(v, 64, axis=1) * sine[...]
-
-    def first_row(n):
-        return lax.broadcasted_iota(I32, (1, 128), 1) + n * 128 - place[0, n : n + 1, :]
 
     def attend(query, head):
         for block in range(2):
@@ -367,15 +367,10 @@
             scores = lax.dot_general(
                 query[rows], kv[0, :seen, :], (((1,), (1,)), ((), ())), preferred_element_type=F32
             ) * (1.0 / HEAD**0.5)
-            i = lax.broadcasted_iota(I32, (256, seen), 0) + block * 256
-            j = lax.broadcasted_iota(I32, (256, seen), 1)
-            starts = jnp.concatenate([first_col[rows, :]] * (seen // 128), axis=1)
-            key_starts = jnp.concatenate([first_row(n) for n in range(seen // 128)], axis=1)
-            allowed = (j <= i) & (starts == key_starts)
-            scores = jnp.where(allowed, scores, NEG)
+            scores = scores + bias[rows, :seen]
             largest = jnp.max(scores, axis=-1, keepdims=True)
-            weight = jnp.where(allowed, jnp.exp(scores - largest), 0.0)
-            probs = (weight / jnp.sum(weight, axis=-1, keepdims=True)).astype(BF16)
+            weight = jnp.exp(scores - largest)
+            probs = (weight * (1.0 / jnp.sum(weight, axis=-1, keepdims=True))).astype(BF16)
             out[rows, head * HEAD : (head + 1) * HEAD] = jnp.dot(
                 probs, kv[1, :seen, :], preferred_element_type=F32
             ).astype(BF16)
@@ -440,8 +435,10 @@
     norm(1)
     weights_whole(0)
     give(0, 0)
+    keep(0, 0)
     weights_whole(1)
     give(1, 0)
+    keep(1, 0)
     weights_pass(3)
     spread_rest(3)
     squares(2)
@@ -454,18 +451,21 @@
     weights_pass(4)
     give(1, 1)
     give(2, 1)
-    keep(0)
+    keep(0, 1)
     weights_whole(3)
     give(3, 0)
     give(3, 1)
-    keep(1)
+    keep(1, 1)
     weights_whole(4)
     give(4, 0)
     give(4, 1)
     keys()
-    keep(2)
-    keep(3)
-    keep(4)
+    keep(2, 0)
+    keep(2, 1)
+    keep(3, 0)
+    keep(3, 1)
+    keep(4, 0)
+    keep(4, 1)
     arrived(kv.at[1 - k], kv_ss, kv_rs)
     attend(rotate(result(1)).astype(BF16), 0)
     attend(rotate(result(2)).astype(BF16), 1)
@@ -523,7 +523,7 @@
             pltpu.VMEM((2 * PART, 128), F32),
             pltpu.VMEM((TOK, 128), F32),
             pltpu.VMEM((TOK, 128), F32),
-            pltpu.VMEM((TOK, 128), I32),
+            pltpu.VMEM((TOK, TOK), F32),
             dma((7,)), dma((7,)), dma((TAB_COPIES,)), dma,
             dma((16, PIECES)), dma((PIECES,)),
             dma((CHUNKS, 6)), dma((CHUNKS, 2)), dma((CHUNKS, 2, 2)),

time: 120 us -> 117 us (0.975)
  Pallas kernels: 117 us -> 114 us
    pallas_call x1, Pallas kernels: 117 us -> 114 us  [on_device(): pl.pallas_call(kernel, out_shape=jax.ShapeDtypeStruct((TOK, 512), BF16),...]
where the time goes in v3:
time: 117 us; the launch traced here: 116 us
  Pallas kernels  114 us (97%)
  local copies, waits for them, and re-layouts  1.87 us (2%)
    pallas_call x1, Pallas kernels, on_device(): pl.pallas_call(kernel, out_shape=jax.ShapeDtypeStruct((TOK, 512), BF16),...  114 us

profile of v3, /device:TPU:0, one launch (start us, length us, event | category | flops | bytes accessed | tf_op | source)
XLA Modules:
  0.0 116.4 jit_solution(6115522849739074106)
XLA Ops:
  0.0 0.6 maximum_bitcast_fusion.frequency
  0.6 113.9 %shard_map.73 = bf16[512,512]{1,0:T(8,128)(2,1)} custom-call(s32[1,4,128]{2,1,0:T(4,128)} %bitcast.6, s32[1,4,128]{2,1,0:T(4,128)} %bitcast.7, f32[1,128]{1,0:T(1,128)} %maximum_bitcast_fusion.frequency, f32[32,1,256]{2,1,0:T(1,128)} %bitcast.5, bf16[9504,512]{1,0:T(8,128)(2,1)} %table.1, bf16[64,8192]{1,0:T(8,128)(2,1)} %wq.1, bf16[64,1024]{1,0:T(8,128)(2,1)} %wk.1, ...), custom_call_target="tpu_custom_call" | custom-call | tf_op jit(solution)/shard_map/pallas_call | solution.py:496
  114.5 1.9 %copy.9 = bf16[512,512]{1,0:T(8,128)(2,1)} copy(bf16[512,512]{1,0:T(8,128)(2,1)} %shard_map.73) | data formatting | bytes 1048576
  (1 shorter events, 0.0 us)
